TPU v7x, 256 devices: a whole 4x4x8 slice. The times are simulated.
256 devices in a mesh: pop: 64 (over x, z, core), mp: 4 (over y).
Axes of the slice: x: 4, y: 4, z: 8, core: 2. Of those that a mesh axis runs over, the one named last changes fastest.
Arguments:
- tokens: bfloat16 [256, 3584], replicated, may hold values from -60 to 60
- target: bfloat16 [256, 3584], P(None, 'mp'), may hold values from -6 to 6
- w_query: bfloat16 [3584, 3584], P('pop', 'mp'), may hold values from -0.09375 to 0.09375
- w_key: bfloat16 [3584, 512], P(None, 'mp'), may hold values from -0.09375 to 0.09375
- w_value: bfloat16 [3584, 512], P(None, 'mp'), may hold values from -0.09375 to 0.09375
- w_out: bfloat16 [3584, 3584], P('mp', 'pop'), may hold values from -0.09375 to 0.09375
- query_left_factors: bfloat16 [64, 3584, 4], P('pop'), may hold values from -0.09375 to 0.09375
- query_right_factors: bfloat16 [64, 4, 3584], P('pop', None, 'mp'), may hold values from -6 to 6
- o_left: bfloat16 [64, 3584, 4], P('pop', 'mp'), may hold values from -0.09375 to 0.09375
- o_right: bfloat16 [64, 4, 3584], P('pop'), may hold values from -6 to 6
- member_ids: int32 [64], P('pop'), may hold values from 0 to 63, each once
Outputs:
- grad_query: float32 [3584, 3584], P('pop', 'mp')
- grad_out: float32 [3584, 3584], P('mp', 'pop')
- fitness: float32 [64], P('pop')
Inputs may be any that keep to these rules, and one draw needn't show every extreme that they name: `member_ids`: every number from 0 to 63 appears once.
All inputs are finite; a program needn't handle non-finite values.
Results may differ from a plain program's by a relative error of at most 0.005.
Values may be sent and summed in bfloat16 or wider, within the bound.
No kernel may reach another device: no remote copies, remote signals or barrier semaphores. Data moves between devices by JAX's collectives and lax.ppermute only.
A program may use at most 64 MiB of HBM per device.

v0:
```python
import math
import jax
import jax.numpy as jnp
from jax import lax
from jax.sharding import Mesh
from jax.sharding import PartitionSpec as P

D = 3584
HEADS = 28
KV_HEADS = 4
HEAD_DIM = 128
RANK = 4
POP = ("pop_0", "pop_1", "pop_2")
noise_scale = 0.5
rope_base = 1000000.0
spread_floor = 0.001


def in_order(parts, dim):
    parts = jnp.moveaxis(parts, 0, dim)
    shape = parts.shape
    return parts.reshape(*shape[:dim], shape[dim] * shape[dim + 1], *shape[dim + 2 :])


def all_blocks(shard, axes, turns):
    parts = shard[None]
    for k in turns:
        parts = lax.all_gather(parts, axes[k], axis=0, tiled=True)
    held = [lax.axis_size(axes[k]) for k in reversed(turns)]
    parts = parts.reshape(*held, *shard.shape)
    turned = sorted(range(len(turns)), key=lambda place: turns[len(turns) - 1 - place])
    return parts.transpose(*turned, *range(len(turns), parts.ndim)).reshape(-1, *shard.shape)


def whole_of(shard, axes, turns, dim):
    return in_order(all_blocks(shard, axes, turns), dim)


def cut_along(shard, dim, devices):
    before, after = (shard.shape[:dim], shard.shape[dim + 1 :])
    return jnp.moveaxis(shard.reshape(*before, devices, -1, *after), dim, 0)


def summed_on_arrival(shard, axis, dim):
    devices = lax.axis_size(axis)
    parts = lax.all_to_all(cut_along(shard, dim, devices), axis, 0, 0, tiled=True)
    return jnp.sum(parts.astype(jnp.float32), axis=0)


def copy_for_each(shard, axis):
    copies = jnp.broadcast_to(shard, (lax.axis_size(axis), *shard.shape))
    return lax.all_to_all(copies, axis, split_axis=0, concat_axis=0, tiled=True)


def of_everyone(shard, axis):
    return copy_for_each(shard, axis).sum(axis=0)


def gathered_copies(shard, axis, dim):
    return in_order(copy_for_each(shard, axis), dim)


def side_by_side(arrays, axis, dim, along):
    columns = [a.reshape(*a.shape[:along], -1) for a in arrays]
    both = jnp.concatenate(columns, axis=along)
    result, at, done = (lax.all_gather(both, axis, axis=dim, tiled=True), 0, [])
    for a, column in zip(arrays, columns):
        share = result[..., at : at + column.shape[along]]
        done.append(share.reshape(*share.shape[:along], *a.shape[along:]))
        at += column.shape[along]
    return tuple(done)


def tables(count, head_size):
    position = jnp.arange(count, dtype=jnp.float32)
    index = jnp.arange(head_size // 2, dtype=jnp.float32)
    freq = jnp.exp(-math.log(rope_base) * 2.0 * index / head_size)
    angle = position[:, None] * freq[None, :]
    return (jnp.cos(angle)[:, None, :], jnp.sin(angle)[:, None, :])


def rotate(field, cosine_table, sine):
    half = field.shape[-1] // 2
    first = field[..., :half]
    second = field[..., half:]
    return jnp.concatenate(
        [first * cosine_table - second * sine, second * cosine_table + first * sine], axis=-1
    )


def per_device(
    tokens,
    target,
    w_query,
    w_key,
    w_value,
    w_out,
    query_left_factors,
    query_right_factors,
    o_left,
    o_right,
    member_ids,
):
    tok = tokens.shape[0]
    local_feats = w_query.shape[1]
    local_kv = w_key.shape[1] // HEAD_DIM
    group = HEADS // KV_HEADS
    local_heads = local_kv * group
    slots = query_left_factors.shape[0]
    scale = HEAD_DIM ** (-0.5)
    cosine_table, sine = tables(tok, HEAD_DIM)
    base = jnp.dot(tokens, whole_of(w_query, POP, (0, 1, 2), 0), preferred_element_type=jnp.float32)
    keys = rotate(
        jnp.dot(tokens, w_key, preferred_element_type=jnp.float32).reshape(tok, local_kv, HEAD_DIM),
        cosine_table,
        sine,
    ).astype(jnp.bfloat16)
    values = (
        jnp.dot(tokens, w_value, preferred_element_type=jnp.float32)
        .astype(jnp.bfloat16)
        .reshape(tok, local_kv, HEAD_DIM)
    )
    signs = (1 - 2 * (member_ids % 2)).astype(jnp.float32)
    factor = noise_scale * signs[:, None, None]
    lowrank_product = jnp.einsum(
        "td,mdr->mtr", tokens, query_left_factors, preferred_element_type=jnp.float32
    ).astype(jnp.bfloat16)
    query = base[None] + factor * jnp.einsum(
        "olj,ojv->olv", lowrank_product, query_right_factors, preferred_element_type=jnp.float32
    )
    query = rotate(
        query.reshape(slots, tok, local_heads, HEAD_DIM), cosine_table[None], sine[None]
    ).astype(jnp.bfloat16)
    query = query.reshape(slots, tok, local_kv, group, HEAD_DIM)
    scores = jnp.einsum("mtkgd,skd->mkgts", query, keys, preferred_element_type=jnp.float32) * scale
    causal = jnp.arange(tok)[:, None] >= jnp.arange(tok)[None, :]
    scores = jnp.where(causal, scores, -1e30)
    probs = jax.nn.softmax(scores, axis=-1).astype(jnp.bfloat16)
    mixed = (
        jnp.einsum("mkgts,skd->mtkgd", probs, values, preferred_element_type=jnp.float32)
        .astype(jnp.bfloat16)
        .reshape(slots, tok, local_feats)
    )
    low_out = jnp.einsum("mtf,mfr->mtr", mixed, o_left, preferred_element_type=jnp.float32)
    right_full = o_right.astype(jnp.float32)
    part = jnp.einsum(
        "mtf,fe->mte",
        mixed,
        lax.all_gather(w_out, POP, axis=1, tiled=True),
        preferred_element_type=jnp.float32,
    )
    term = part + factor * jnp.einsum(
        "mtr,mre->mte", low_out, right_full, precision=lax.Precision.HIGHEST
    )
    output = summed_on_arrival(term.astype(jnp.bfloat16), "mp", 2)
    diff = output - target.astype(jnp.float32)[None]
    errors = of_everyone(jnp.sum(diff * diff, axis=(1, 2)), "mp")
    fitness = -(errors / (tok * D))
    count = slots * lax.axis_size(POP)
    everyone = gathered_copies(fitness, POP, 0)
    mean = jnp.sum(everyone) / count
    spread = jnp.sum((everyone - mean) * (everyone - mean)) / count
    weight = signs * (fitness - mean) / jnp.sqrt(spread + spread_floor)
    every_weight = gathered_copies(weight, POP, 0)
    right_factors_gathered, left_all = side_by_side((query_right_factors, o_left), POP, 0, 1)
    rows_q = lax.all_to_all(query_left_factors, POP, split_axis=1, concat_axis=0, tiled=True)
    cols_o = lax.all_to_all(o_right, POP, split_axis=2, concat_axis=0, tiled=True)
    whole_population = rows_q.shape[0]
    left_q = jnp.transpose(
        rows_q.astype(jnp.float32) * every_weight[:, None, None], (1, 0, 2)
    ).reshape(rows_q.shape[1], whole_population * RANK)
    right_q = right_factors_gathered.astype(jnp.float32).reshape(
        whole_population * RANK, local_feats
    )
    grad_query = jnp.dot(left_q, right_q, precision=lax.Precision.HIGHEST) / noise_scale
    output_left_factor = jnp.transpose(
        left_all.astype(jnp.float32) * every_weight[:, None, None], (1, 0, 2)
    ).reshape(local_feats, whole_population * RANK)
    right_o = cols_o.astype(jnp.float32).reshape(whole_population * RANK, cols_o.shape[2])
    grad_out = jnp.dot(output_left_factor, right_o, precision=lax.Precision.HIGHEST) / noise_scale
    return (grad_query, grad_out, fitness)


def solution(mesh):
    torus = Mesh(mesh.devices.reshape(4, 8, 2, mesh.shape["mp"]), ("pop_0", "pop_1", "pop_2", "mp"))
    placed = (
        P(),
        P(None, "mp"),
        P(POP, "mp"),
        P(None, "mp"),
        P(None, "mp"),
        P("mp", POP),
        P(POP, None, None),
        P(POP, None, "mp"),
        P(POP, "mp", None),
        P(POP, None, None),
        P(POP),
    )
    return jax.shard_map(
        per_device,
        mesh=torus,
        in_specs=placed,
        out_specs=(P(POP, "mp"), P("mp", POP), P(POP)),
        check_vma=False,
    )
```

profile of v0, /device:TPU:1, one launch (start us, length us, event | category | flops | bytes accessed | tf_op | source)
XLA Modules:
  0.0 428.7 jit_solution(7784847421207332163)
XLA Ops:
  7.2 13.0 %all-gather = bf16[224,896]{1,0:T(8,128)(2,1)} all-gather(bf16[56,896]{1,0:T(8,128)(2,1)} %param.13), channel_id=2, replica_groups=mesh['pop_0'=4,'pop_1'=8,'pop_2'=2,'mp'=4] {'pop_0'}, dimensions={0}, use_global_device_ids=true | all-gather | bytes 501760 | tf_op jit(solution)/shard_map/all_gather | solution.py:28
  20.3 49.6 %all-gather.6.cloned.1.call-done = bf16[32,56,896]{2,1,0:T(8,128)(2,1)} async-done(((bf16[4,56,896]{2,1,0:T(8,128)(2,1)}), bf16[32,56,896]{2,1,0:T(8,128)(2,1)}) %all-gather.6.cloned.1.call-update) | async-done | bytes 3211280 | tf_op jit(solution)/shard_map/all_gather | solution.py:28
  73.6 19.9 %all-gather.8.cloned.1.call-done = bf16[64,56,896]{2,1,0:T(8,128)(2,1)} async-done(((bf16[32,56,896]{2,1,0:T(8,128)(2,1)}), bf16[64,56,896]{2,1,0:T(8,128)(2,1)}) %all-gather.8.cloned.1.call-update) | async-done | bytes 6422544 | tf_op jit(solution)/shard_map/all_gather | solution.py:28
  93.5 3.3 copy.114
  96.9 2.1 fusion.29
  99.1 2.1 fusion.3
  101.1 1.5 copy.115
  110.0 2.6 convolution_convert_fusion
  112.8 65.1 %all-gather.10.cloned.1.call-done = bf16[896,3584]{0,1:T(8,128)(2,1)} async-done(((bf16[896,56]{0,1:T(8,128)(2,1)}), bf16[896,3584]{0,1:T(8,128)(2,1)}) %all-gather.10.cloned.1.call-update) | async-done | bytes 6422544 | tf_op jit(solution)/shard_map/all_gather | solution.py:149
  177.9 4.9 %fusion.30 = f32[256,3584]{1,0:T(8,128)S(1)} fusion(bf16[256,896]{0,1:T(8,128)(2,1)S(1)} %bitcast.106, bf16[896,3584]{0,1:T(8,128)(2,1)} %all-gather.10.cloned.1.call-done), kind=kOutput, calls=%fused_computation.58 | convolution fusion | flops 1644167168 | bytes 10551296 | tf_op jit(solution)/shard_map/mtf,fe->mte/dot_general | solution.py:146
  182.8 3.1 fusion.1
  185.9 3.3 reshape.288
  189.2 1.5 copy.145
  190.7 4.0 all-to-all-start.1
  195.3 22.5 %all-to-all-done.1 = bf16[4,1,256,896]{3,2,1,0:T(8,128)(2,1)S(1)} async-done(((bf16[4,1,256,896]{3,2,1,0:T(8,128)(2,1)}), bf16[4,1,256,896]{3,2,1,0:T(8,128)(2,1)S(1)}, u32[]{:S(2)}, u32[]{:S(2)}) %all-to-all-start.1) | async-done | bytes 1835040 | tf_op jit(solution)/shard_map/all_to_all | solution.py:46
  219.6 6.5 %all_to_all.47 = f32[4,1,1]{2,1,0:T(1,128)S(1)} all-to-all(f32[4,1,1]{2,1,0:T(1,128)S(1)} %broadcast_in_dim.34), channel_id=1, replica_groups=mesh['pop_0'=4,'pop_1'=8,'pop_2'=2,'mp'=4] {'mp'}, dimensions={0} | all-to-all | bytes 32 | tf_op jit(solution)/shard_map/all_to_all | solution.py:52
  227.9 7.9 %all-to-all-start.3 = ((f32[64,1,1]{2,1,0:T(1,128)}), f32[64,1,1]{2,1,0:T(1,128)S(1)}, u32[]{:S(2)}, u32[]{:S(2)}) async-start(f32[64,1,1]{2,1,0:T(1,128)} %broadcast_in_dim.35), calls=%async_computation.3 | async-start | bytes 65536 | tf_op jit(solution)/shard_map/all_to_all | solution.py:52
  235.9 51.8 %all-gather.1 = bf16[64,1,7168]{2,1,0:T(2,128)(2,1)S(1)} all-gather(bf16[1,1,7168]{2,1,0:T(2,128)(2,1)S(1)} %maximum_bitcast_fusion.2), channel_id=1, replica_groups=mesh['pop_0'=4,'pop_1'=8,'pop_2'=2,'mp'=4] {'pop_0','pop_1','pop_2'}, dimensions={0}, use_global_device_ids=true | all-gather | bytes 931840 | tf_op jit(solution)/shard_map/all_gather | solution.py:66
  287.7 3.2 copy.129
  292.2 7.3 %all-to-all-start.5 = ((bf16[1,4,3584]{1,0,2:T(2,128)(2,1)}), bf16[1,4,3584]{1,0,2:T(2,128)(2,1)S(1)}, u32[]{:S(2)}, u32[]{:S(2)}) async-start(bf16[1,4,3584]{1,0,2:T(2,128)(2,1)} %copy.129), calls=%async_computation.5 | async-start | bytes 3670016 | tf_op jit(solution)/shard_map/all_to_all | solution.py:167
  299.4 2.0 slice_convert_fusion
  301.5 3.2 copy.112
  306.1 38.7 %all-to-all-done.5 = bf16[1,4,3584]{1,0,2:T(2,128)(2,1)S(1)} async-done(((bf16[1,4,3584]{1,0,2:T(2,128)(2,1)}), bf16[1,4,3584]{1,0,2:T(2,128)(2,1)S(1)}, u32[]{:S(2)}, u32[]{:S(2)}) %all-to-all-start.5) | async-done | bytes 28704 | tf_op jit(solution)/shard_map/all_to_all | solution.py:167
  344.8 6.2 %all-to-all-start = ((bf16[1,3584,4]{2,0,1:T(2,128)(2,1)}), bf16[1,3584,4]{2,0,1:T(2,128)(2,1)}, u32[]{:S(2)}, u32[]{:S(2)}) async-start(bf16[1,3584,4]{2,0,1:T(2,128)(2,1)} %copy.112), calls=%async_computation | async-start | bytes 3670016 | tf_op jit(solution)/shard_map/all_to_all | solution.py:166
  352.3 44.0 %all-to-all-done = bf16[1,3584,4]{2,0,1:T(2,128)(2,1)} async-done(((bf16[1,3584,4]{2,0,1:T(2,128)(2,1)}), bf16[1,3584,4]{2,0,1:T(2,128)(2,1)}, u32[]{:S(2)}, u32[]{:S(2)}) %all-to-all-start) | async-done | bytes 28704 | tf_op jit(solution)/shard_map/all_to_all | solution.py:166
  396.9 6.0 %all-to-all-start.4 = ((f32[64,1,1]{2,1,0:T(1,128)}), f32[64,1,1]{2,1,0:T(1,128)S(1)}, u32[]{:S(2)}, u32[]{:S(2)}) async-start(f32[64,1,1]{2,1,0:T(1,128)} %broadcast_in_dim.36), calls=%async_computation.4 | async-start | bytes 65536 | tf_op jit(solution)/shard_map/all_to_all | solution.py:52
  403.0 1.8 copy.127
  406.0 1.8 copy.130
  408.1 3.7 copy.113
  412.8 1.6 multiply_bitcast_fusion
  414.4 2.8 copy.128
  417.2 1.5 reshape.293
  (71 shorter events, 22.1 us)
Async XLA Ops:
  7.2 64.2 %copy-start = (bf16[256,3584]{1,0:T(8,128)(2,1)S(1)}, bf16[256,3584]{1,0:T(8,128)(2,1)}, u32[]{:S(2)}) copy-start(bf16[256,3584]{1,0:T(8,128)(2,1)} %param.11) | copy-start | bytes 5505028
  7.2 62.7 %all-gather.6.cloned.1.call-start = ((), (), s32[]{:S(2)}) async-start(), calls=%async_computation.6 | async-start | bytes 3612672 | tf_op jit(solution)/shard_map/all_gather | solution.py:28
  20.2 51.2 %copy-start.4 = (bf16[3584,128]{1,0:T(8,128)(2,1)S(1)}, bf16[3584,128]{1,0:T(8,128)(2,1)}, u32[]{:S(2)}) copy-start(bf16[3584,128]{1,0:T(8,128)(2,1)} %param.14) | copy-start | bytes 2752516
  20.3 73.3 %all-gather.8.cloned.1.call-start = ((), (), s32[]{:S(2)}) async-start(), calls=%async_computation.7 | async-start | bytes 9633792 | tf_op jit(solution)/shard_map/all_gather | solution.py:28
  69.9 107.9 %all-gather.10.cloned.1.call-start = ((), (), s32[]{:S(2)}) async-start(), calls=%async_computation.8 | async-start | bytes 6522880 | tf_op jit(solution)/shard_map/all_gather | solution.py:149
  96.9 2.2 copy-start.9
  96.9 2.2 copy-start.11
  106.1 1.4 copy-start.6
  106.1 1.4 copy-start.7
  108.1 1.3 copy-start.2
  108.2 1.9 copy-start.13
  110.0 2.6 copy-start.12
  112.8 70.0 %copy-start.8 = (bf16[1,4,3584]{2,1,0:T(4,128)(2,1)S(1)}, bf16[1,4,3584]{2,1,0:T(4,128)(2,1)}, u32[]{:S(2)}) copy-start(bf16[1,4,3584]{2,1,0:T(4,128)(2,1)} %param.20) | copy-start | bytes 86020
  190.7 27.1 %all-to-all-start.1 = ((bf16[4,1,256,896]{3,2,1,0:T(8,128)(2,1)}), bf16[4,1,256,896]{3,2,1,0:T(8,128)(2,1)S(1)}, u32[]{:S(2)}, u32[]{:S(2)}) async-start(bf16[4,1,256,896]{3,2,1,0:T(8,128)(2,1)} %bitcast.98), calls=%async_computation.1 | async-start | bytes 3670016 | tf_op jit(solution)/shard_map/all_to_all | solution.py:46
  194.7 23.3 %copy-start.5 = (bf16[256,896]{1,0:T(8,128)(2,1)S(1)}, bf16[256,896]{1,0:T(8,128)(2,1)}, u32[]{:S(2)}) copy-start(bf16[256,896]{1,0:T(8,128)(2,1)} %param.12) | copy-start | bytes 1376260
  227.9 64.2 %all-to-all-start.3 = ((f32[64,1,1]{2,1,0:T(1,128)}), f32[64,1,1]{2,1,0:T(1,128)S(1)}, u32[]{:S(2)}, u32[]{:S(2)}) async-start(f32[64,1,1]{2,1,0:T(1,128)} %broadcast_in_dim.35), calls=%async_computation.3 | async-start | bytes 65536 | tf_op jit(solution)/shard_map/all_to_all | solution.py:52
  292.2 52.6 %all-to-all-start.5 = ((bf16[1,4,3584]{1,0,2:T(2,128)(2,1)}), bf16[1,4,3584]{1,0,2:T(2,128)(2,1)S(1)}, u32[]{:S(2)}, u32[]{:S(2)}) async-start(bf16[1,4,3584]{1,0,2:T(2,128)(2,1)} %copy.129), calls=%async_computation.5 | async-start | bytes 3670016 | tf_op jit(solution)/shard_map/all_to_all | solution.py:167
  299.4 2.1 copy-start.10
  344.8 51.5 %all-to-all-start = ((bf16[1,3584,4]{2,0,1:T(2,128)(2,1)}), bf16[1,3584,4]{2,0,1:T(2,128)(2,1)}, u32[]{:S(2)}, u32[]{:S(2)}) async-start(bf16[1,3584,4]{2,0,1:T(2,128)(2,1)} %copy.112), calls=%async_computation | async-start | bytes 3670016 | tf_op jit(solution)/shard_map/all_to_all | solution.py:166
  396.9 15.3 %all-to-all-start.4 = ((f32[64,1,1]{2,1,0:T(1,128)}), f32[64,1,1]{2,1,0:T(1,128)S(1)}, u32[]{:S(2)}, u32[]{:S(2)}) async-start(f32[64,1,1]{2,1,0:T(1,128)} %broadcast_in_dim.36), calls=%async_computation.4 | async-start | bytes 65536 | tf_op jit(solution)/shard_map/all_to_all | solution.py:52
  407.9 4.9 %copy-start.3 = (f32[64,3584]{0,1:T(8,128)S(1)}, f32[64,3584]{0,1:T(8,128)}, u32[]{:S(2)}) copy-start(f32[64,3584]{0,1:T(8,128)} %copy.127) | copy-start | bytes 2752516
  414.3 6.7 %copy-start.1 = (bf16[256,3584]{1,0:T(8,128)(2,1)S(1)}, bf16[256,3584]{1,0:T(8,128)(2,1)}, u32[]{:S(2)}) copy-start(bf16[256,3584]{1,0:T(8,128)(2,1)} %param.11) | copy-start | bytes 5505028
Sparse Core Ops, SparseCore 0:
  20.4 49.4 all-gather.5
  71.7 21.7 all-gather.7
  96.2 81.5 all-gather.9
where the time goes:
time: 430 us; the launch traced here: 429 us
  waiting for transfers between devices  241 us (56%)
  blocking collectives  71.3 us (17%)
  local copies, waits for them, and re-layouts  38.2 us (9%)
  starting transfers between devices  31.5 us (7%)
  matrix products  18.6 us (4%)
  between operations  17.9 us (4%)
  other arithmetic  10.5 us (2%)
    all_gather x2, waiting for transfers between devices, all_blocks(): parts = lax.all_gather(parts, axes[k], axis=0, tiled=True)  69.5 us
    all_gather x1, waiting for transfers between devices, per_device(): lax.all_gather(w_out, POP, axis=1, tiled=True)  65.1 us
    all_gather x1, blocking collectives, side_by_side(): result, at, done = (lax.all_gather(both, axis, axis=dim, tiled=True), 0, [])  51.8 us
    all_to_all x1, waiting for transfers between devices, per_device(): lax.all_to_all(query_left_factors, POP, split_axis=1, concat_axis=0, tile...  44 us
    all_to_all x1, waiting for transfers between devices, per_device(): lax.all_to_all(o_right, POP, split_axis=2, concat_axis=0, tiled=True)  38.7 us
    all_to_all x1, waiting for transfers between devices, summed_on_arrival(): lax.all_to_all(cut_along(shard, dim, devices), axis, 0, 0, tiled=True)  22.5 us
    all_to_all x2, starting transfers between devices, copy_for_each(): return lax.all_to_all(copies, axis, split_axis=0, concat_axis=0, tiled=True)  14 us
    all_gather x1, blocking collectives, all_blocks(): parts = lax.all_gather(parts, axes[k], axis=0, tiled=True)  13 us
  transfers between devices with their start and end apart: 8, of which 7 were waited for; matrix products, arithmetic and copies ran while one was open for 9% of the time, Pallas kernels for 0%

commit v1 on v0

--- a/solution.py
+++ b/solution.py
@@ -101,6 +101,10 @@
     o_right,
     member_ids,
 ):
+
+    def recover_the_weights(piece_in, dim_k):
+        return jnp.concatenate(lax.all_gather(piece_in, axis_name=POP), axis=dim_k)
+
     tok = tokens.shape[0]
     local_feats = w_query.shape[1]
     local_kv = w_key.shape[1] // HEAD_DIM
@@ -146,7 +150,7 @@
     part = jnp.einsum(
         "mtf,fe->mte",
         mixed,
-        lax.all_gather(w_out, POP, axis=1, tiled=True),
+        recover_the_weights(w_out, dim_k=1),
         preferred_element_type=jnp.float32,
     )
     term = part + factor * jnp.einsum(

time: 430 us -> 436 us (1.014)
  local copies, waits for them, and re-layouts: 38.2 us -> 45.9 us
    unnamed x35 -> x36, local copies, waits for them, and re-layouts: 12 us -> 16.1 us
where the time goes in v1:
time: 436 us; the launch traced here: 435 us
  waiting for transfers between devices  241 us (55%)
  blocking collectives  71.3 us (16%)
  local copies, waits for them, and re-layouts  45.9 us (11%)
  starting transfers between devices  31.9 us (7%)
  between operations  18 us (4%)
  matrix products  16 us (4%)
  other arithmetic  10.5 us (2%)
    all_gather x2, waiting for transfers between devices, all_blocks(): parts = lax.all_gather(parts, axes[k], axis=0, tiled=True)  69.5 us
    all_gather x1, waiting for transfers between devices, recover_the_weights(): return jnp.concatenate(lax.all_gather(piece_in, axis_name=POP), axis=dim_k)  65.4 us
    all_gather x1, blocking collectives, side_by_side(): result, at, done = (lax.all_gather(both, axis, axis=dim, tiled=True), 0, [])  51.8 us
    all_to_all x1, waiting for transfers between devices, per_device(): lax.all_to_all(query_left_factors, POP, split_axis=1, concat_axis=0, tile...  44 us
    all_to_all x1, waiting for transfers between devices, per_device(): lax.all_to_all(o_right, POP, split_axis=2, concat_axis=0, tiled=True)  38.7 us
    all_to_all x1, waiting for transfers between devices, summed_on_arrival(): lax.all_to_all(cut_along(shard, dim, devices), axis, 0, 0, tiled=True)  22.5 us
    unnamed x36, local copies, waits for them, and re-layouts  16.1 us
    all_to_all x2, starting transfers between devices, copy_for_each(): return lax.all_to_all(copies, axis, split_axis=0, concat_axis=0, tiled=True)  14.4 us
  transfers between devices with their start and end apart: 8, of which 7 were waited for; matrix products, arithmetic and copies ran while one was open for 9% of the time, Pallas kernels for 0%

profile of v1, /device:TPU:1, one launch (start us, length us, event | category | flops | bytes accessed | tf_op | source)
XLA Modules:
  0.0 434.6 jit_solution(13605954745094671707)
XLA Ops:
  7.2 13.0 %all-gather = bf16[224,896]{1,0:T(8,128)(2,1)} all-gather(bf16[56,896]{1,0:T(8,128)(2,1)} %param.13), channel_id=2, replica_groups=mesh['pop_0'=4,'pop_1'=8,'pop_2'=2,'mp'=4] {'pop_0'}, dimensions={0}, use_global_device_ids=true | all-gather | bytes 501760 | tf_op jit(solution)/shard_map/all_gather | solution.py:28
  20.3 49.6 %all-gather.7.cloned.1.call-done = bf16[32,56,896]{2,1,0:T(8,128)(2,1)} async-done(((bf16[4,56,896]{2,1,0:T(8,128)(2,1)}), bf16[32,56,896]{2,1,0:T(8,128)(2,1)}) %all-gather.7.cloned.1.call-update) | async-done | bytes 3211280 | tf_op jit(solution)/shard_map/all_gather | solution.py:28
  73.6 19.9 %all-gather.9.cloned.1.call-done = bf16[64,56,896]{2,1,0:T(8,128)(2,1)} async-done(((bf16[32,56,896]{2,1,0:T(8,128)(2,1)}), bf16[64,56,896]{2,1,0:T(8,128)(2,1)}) %all-gather.9.cloned.1.call-update) | async-done | bytes 6422544 | tf_op jit(solution)/shard_map/all_gather | solution.py:28
  93.5 3.3 copy.119
  96.9 2.1 fusion.29
  99.1 2.1 fusion.3
  110.0 2.6 convolution_convert_fusion
  112.8 65.4 %all-gather.11.cloned.1.call-done = bf16[57344,56]{0,1:T(8,128)(2,1)} async-done(((bf16[896,56]{0,1:T(8,128)(2,1)}), bf16[57344,56]{0,1:T(8,128)(2,1)}) %all-gather.11.cloned.1.call-update) | async-done | bytes 6422544 | tf_op jit(solution)/shard_map/all_gather | solution.py:106
  178.1 4.0 copy.148
  182.2 3.7 copy.126
  185.9 2.4 fusion.30
  188.2 3.1 fusion.1
  191.3 3.3 reshape.296
  194.7 1.5 copy.152
  196.2 4.0 all-to-all-start.1
  200.7 22.5 %all-to-all-done.1 = bf16[4,1,256,896]{3,2,1,0:T(8,128)(2,1)S(1)} async-done(((bf16[4,1,256,896]{3,2,1,0:T(8,128)(2,1)}), bf16[4,1,256,896]{3,2,1,0:T(8,128)(2,1)S(1)}, u32[]{:S(2)}, u32[]{:S(2)}) %all-to-all-start.1) | async-done | bytes 1835040 | tf_op jit(solution)/shard_map/all_to_all | solution.py:46
  225.0 6.5 %all_to_all.47 = f32[4,1,1]{2,1,0:T(1,128)S(1)} all-to-all(f32[4,1,1]{2,1,0:T(1,128)S(1)} %broadcast_in_dim.34), channel_id=1, replica_groups=mesh['pop_0'=4,'pop_1'=8,'pop_2'=2,'mp'=4] {'mp'}, dimensions={0} | all-to-all | bytes 32 | tf_op jit(solution)/shard_map/all_to_all | solution.py:52
  233.4 8.1 %all-to-all-start.3 = ((f32[64,1,1]{2,1,0:T(1,128)}), f32[64,1,1]{2,1,0:T(1,128)S(1)}, u32[]{:S(2)}, u32[]{:S(2)}) async-start(f32[64,1,1]{2,1,0:T(1,128)} %broadcast_in_dim.35), calls=%async_computation.3 | async-start | bytes 65536 | tf_op jit(solution)/shard_map/all_to_all | solution.py:52
  241.5 51.8 %all-gather.2 = bf16[64,1,7168]{2,1,0:T(2,128)(2,1)S(1)} all-gather(bf16[1,1,7168]{2,1,0:T(2,128)(2,1)S(1)} %maximum_bitcast_fusion.2), channel_id=1, replica_groups=mesh['pop_0'=4,'pop_1'=8,'pop_2'=2,'mp'=4] {'pop_0','pop_1','pop_2'}, dimensions={0}, use_global_device_ids=true | all-gather | bytes 931840 | tf_op jit(solution)/shard_map/all_gather | solution.py:66
  293.3 3.2 copy.135
  297.8 7.3 %all-to-all-start.5 = ((bf16[1,4,3584]{1,0,2:T(2,128)(2,1)}), bf16[1,4,3584]{1,0,2:T(2,128)(2,1)S(1)}, u32[]{:S(2)}, u32[]{:S(2)}) async-start(bf16[1,4,3584]{1,0,2:T(2,128)(2,1)} %copy.135), calls=%async_computation.5 | async-start | bytes 3670016 | tf_op jit(solution)/shard_map/all_to_all | solution.py:171
  305.0 2.0 slice_convert_fusion
  307.1 3.2 copy.117
  311.7 38.7 %all-to-all-done.5 = bf16[1,4,3584]{1,0,2:T(2,128)(2,1)S(1)} async-done(((bf16[1,4,3584]{1,0,2:T(2,128)(2,1)}), bf16[1,4,3584]{1,0,2:T(2,128)(2,1)S(1)}, u32[]{:S(2)}, u32[]{:S(2)}) %all-to-all-start.5) | async-done | bytes 28704 | tf_op jit(solution)/shard_map/all_to_all | solution.py:171
  350.4 6.2 %all-to-all-start = ((bf16[1,3584,4]{2,0,1:T(2,128)(2,1)}), bf16[1,3584,4]{2,0,1:T(2,128)(2,1)}, u32[]{:S(2)}, u32[]{:S(2)}) async-start(bf16[1,3584,4]{2,0,1:T(2,128)(2,1)} %copy.117), calls=%async_computation | async-start | bytes 3670016 | tf_op jit(solution)/shard_map/all_to_all | solution.py:170
  357.9 44.0 %all-to-all-done = bf16[1,3584,4]{2,0,1:T(2,128)(2,1)} async-done(((bf16[1,3584,4]{2,0,1:T(2,128)(2,1)}), bf16[1,3584,4]{2,0,1:T(2,128)(2,1)}, u32[]{:S(2)}, u32[]{:S(2)}) %all-to-all-start) | async-done | bytes 28704 | tf_op jit(solution)/shard_map/all_to_all | solution.py:170
  402.5 6.2 %all-to-all-start.4 = ((f32[64,1,1]{2,1,0:T(1,128)}), f32[64,1,1]{2,1,0:T(1,128)S(1)}, u32[]{:S(2)}, u32[]{:S(2)}) async-start(f32[64,1,1]{2,1,0:T(1,128)} %broadcast_in_dim.36), calls=%async_computation.4 | async-start | bytes 65536 | tf_op jit(solution)/shard_map/all_to_all | solution.py:52
  408.8 1.8 copy.133
  411.9 1.8 copy.136
  413.9 3.7 copy.118
  418.6 1.6 multiply_bitcast_fusion
  420.2 2.8 copy.134
  (73 shorter events, 25.1 us)
Async XLA Ops:
  7.2 64.2 %copy-start = (bf16[256,3584]{1,0:T(8,128)(2,1)S(1)}, bf16[256,3584]{1,0:T(8,128)(2,1)}, u32[]{:S(2)}) copy-start(bf16[256,3584]{1,0:T(8,128)(2,1)} %param.11) | copy-start | bytes 5505028
  7.2 62.7 %all-gather.7.cloned.1.call-start = ((), (), s32[]{:S(2)}) async-start(), calls=%async_computation.6 | async-start | bytes 3612672 | tf_op jit(solution)/shard_map/all_gather | solution.py:28
  20.2 51.2 %copy-start.4 = (bf16[3584,128]{1,0:T(8,128)(2,1)S(1)}, bf16[3584,128]{1,0:T(8,128)(2,1)}, u32[]{:S(2)}) copy-start(bf16[3584,128]{1,0:T(8,128)(2,1)} %param.14) | copy-start | bytes 2752516
  20.3 73.3 %all-gather.9.cloned.1.call-start = ((), (), s32[]{:S(2)}) async-start(), calls=%async_computation.7 | async-start | bytes 9633792 | tf_op jit(solution)/shard_map/all_gather | solution.py:28
  69.9 108.2 %all-gather.11.cloned.1.call-start = ((), (), s32[]{:S(2)}) async-start(), calls=%async_computation.8 | async-start | bytes 6522880 | tf_op jit(solution)/shard_map/all_gather | solution.py:106
  96.9 2.2 copy-start.9
  96.9 2.2 copy-start.11
  106.1 1.4 copy-start.6
  106.1 1.4 copy-start.7
  108.1 1.3 copy-start.2
  108.2 1.8 copy-start.13
  110.0 2.6 copy-start.12
  185.9 2.4 copy-start.8
  196.2 27.1 %all-to-all-start.1 = ((bf16[4,1,256,896]{3,2,1,0:T(8,128)(2,1)}), bf16[4,1,256,896]{3,2,1,0:T(8,128)(2,1)S(1)}, u32[]{:S(2)}, u32[]{:S(2)}) async-start(bf16[4,1,256,896]{3,2,1,0:T(8,128)(2,1)} %bitcast.105), calls=%async_computation.1 | async-start | bytes 3670016 | tf_op jit(solution)/shard_map/all_to_all | solution.py:46
  200.2 23.3 %copy-start.5 = (bf16[256,896]{1,0:T(8,128)(2,1)S(1)}, bf16[256,896]{1,0:T(8,128)(2,1)}, u32[]{:S(2)}) copy-start(bf16[256,896]{1,0:T(8,128)(2,1)} %param.12) | copy-start | bytes 1376260
  233.4 64.4 %all-to-all-start.3 = ((f32[64,1,1]{2,1,0:T(1,128)}), f32[64,1,1]{2,1,0:T(1,128)S(1)}, u32[]{:S(2)}, u32[]{:S(2)}) async-start(f32[64,1,1]{2,1,0:T(1,128)} %broadcast_in_dim.35), calls=%async_computation.3 | async-start | bytes 65536 | tf_op jit(solution)/shard_map/all_to_all | solution.py:52
  297.8 52.7 %all-to-all-start.5 = ((bf16[1,4,3584]{1,0,2:T(2,128)(2,1)}), bf16[1,4,3584]{1,0,2:T(2,128)(2,1)S(1)}, u32[]{:S(2)}, u32[]{:S(2)}) async-start(bf16[1,4,3584]{1,0,2:T(2,128)(2,1)} %copy.135), calls=%async_computation.5 | async-start | bytes 3670016 | tf_op jit(solution)/shard_map/all_to_all | solution.py:171
  305.0 2.1 copy-start.10
  350.4 51.5 %all-to-all-start = ((bf16[1,3584,4]{2,0,1:T(2,128)(2,1)}), bf16[1,3584,4]{2,0,1:T(2,128)(2,1)}, u32[]{:S(2)}, u32[]{:S(2)}) async-start(bf16[1,3584,4]{2,0,1:T(2,128)(2,1)} %copy.117), calls=%async_computation | async-start | bytes 3670016 | tf_op jit(solution)/shard_map/all_to_all | solution.py:170
  402.5 15.5 %all-to-all-start.4 = ((f32[64,1,1]{2,1,0:T(1,128)}), f32[64,1,1]{2,1,0:T(1,128)S(1)}, u32[]{:S(2)}, u32[]{:S(2)}) async-start(f32[64,1,1]{2,1,0:T(1,128)} %broadcast_in_dim.36), calls=%async_computation.4 | async-start | bytes 65536 | tf_op jit(solution)/shard_map/all_to_all | solution.py:52
  413.7 4.9 %copy-start.3 = (f32[64,3584]{0,1:T(8,128)S(1)}, f32[64,3584]{0,1:T(8,128)}, u32[]{:S(2)}) copy-start(f32[64,3584]{0,1:T(8,128)} %copy.133) | copy-start | bytes 2752516
  420.2 6.7 %copy-start.1 = (bf16[256,3584]{1,0:T(8,128)(2,1)S(1)}, bf16[256,3584]{1,0:T(8,128)(2,1)}, u32[]{:S(2)}) copy-start(bf16[256,3584]{1,0:T(8,128)(2,1)} %param.11) | copy-start | bytes 5505028
Sparse Core Ops, SparseCore 0:
  20.4 49.4 all-gather.6
  71.7 21.7 all-gather.8
  96.2 81.8 all-gather.10
